TPU v7x, 32 devices: a whole 2x2x4 slice. The times are simulated.
32 devices in a mesh: groups: 2 (over y), seq: 4 (over z), head: 2 (over x), rep: 2 (over core).
Axes of the slice: x: 2, y: 2, z: 4, core: 2. Of those that a mesh axis runs over, the one named last changes fastest.
Arguments:
- queries: bfloat16 [2048, 6144], P(('groups', 'seq', 'rep'), 'head'), parts along dimension 0, may hold values from -150 to 150
- key_tokens: bfloat16 [2048, 6144], P(('groups', 'seq', 'rep'), 'head'), parts along dimension 0, may hold values from -6 to 6
- value_tokens: bfloat16 [2048, 6144], P(('groups', 'seq', 'rep'), 'head'), parts along dimension 0, may hold values from -6 to 6
- stream: bfloat16 [2048, 6144], P(('groups', 'seq', 'rep'), 'head'), parts along dimension 0, may hold values from -6 to 6
- norm_gain: float32 [6144], P('head'), may hold values from 0.1 to 1.9
- latent_weight: bfloat16 [6144, 64], P('head'), may hold values from -0.078125 to 0.078125
- tile_pool: bfloat16 [8, 64, 2, 128], P(('groups', 'seq')), parts along dimension 0, may hold values from -6 to 6
- tile_position: int32 [8], P('groups'), parts along dimension 0, may hold values from 0 to 3, each once
- lift_weight: bfloat16 [64, 512], P(None, ('head', 'rep')), may hold values from -0.75 to 0.75
- lift_bias: float32 [512], P(('head', 'rep')), may hold values from -3 to 3
- conv_weight: bfloat16 [2, 27, 512, 512], P(None, None, ('head', 'rep')), may hold values from -0.0546875 to 0.0546875
Outputs:
- hidden: bfloat16 [2048, 6144], P(('groups', 'seq', 'rep'), 'head'), parts along dimension 0
- latents: float32 [2048, 64], P(('groups', 'seq', 'rep')), parts along dimension 0
- decoded: float32 [1024, 2, 4, 128], P(('groups', 'head', 'rep'), None, 'seq'), parts along dimension 0
There are 2 independent parts, one for each index of `groups`. A program takes and returns all parts, laid end to end along the dimension named above; an argument that names none is the same for every part. Nothing has to cross between parts.
Inputs may be any that keep to these rules, and one draw needn't show every extreme that they name: `tile_position`: each of the 4 grid rows is named by exactly one pool tile.
All inputs are finite; a program needn't handle non-finite values.
Results may differ from a plain program's by a relative error of at most 0.01.
Values may be sent and summed in bfloat16 or wider, within the bound.
No kernel may reach another device: no remote copies, remote signals or barrier semaphores. Data moves between devices by JAX's collectives and lax.ppermute only.
A program may use at most 128 MiB of HBM per device.

v0:
```python
import math

import jax
import jax.numpy as jnp
from jax import lax
from jax.experimental import pallas as pl
from jax.experimental.pallas import tpu as pltpu
from jax.sharding import PartitionSpec as P

HEAD_DIM = 128
WIDTH = 6144


epsilon = 1e-06
negative = -1e30


def padded(shard, sides, width):
    for axis, dim in sides:
        peers, length = (lax.axis_size(axis), shard.shape[dim])
        up = [(i, (i + 1) % peers) for i in range(peers - 1)]
        down = [(j, i) for i, j in up]
        last = lax.slice_in_dim(shard, length - width, length, axis=dim)
        leading = lax.slice_in_dim(shard, 0, width, axis=dim)
        before = lax.ppermute(last, axis, up)
        after = lax.ppermute(leading, axis, down)
        shard = jnp.concatenate([before, shard, after], axis=dim)
    return shard


def prepare(block_rows):
    row_count = block_rows.shape[0]
    head_count = block_rows.shape[1] // HEAD_DIM
    query_heads = block_rows.reshape(row_count, head_count, HEAD_DIM)
    initial = (
        jnp.full((head_count, row_count), negative, jnp.float32),
        jnp.zeros((head_count, row_count), jnp.float32),
        jnp.zeros((head_count, row_count, HEAD_DIM), jnp.float32),
    )
    return (query_heads, initial)


def make_update(query_heads, state, pieces):
    head_count = query_heads.shape[1]
    factor = 1.0 / math.sqrt(HEAD_DIM)
    running_max, running_sum, accum = state
    key_piece, value_piece = pieces
    piece_rows = key_piece.shape[0]
    key_heads = key_piece.reshape(piece_rows, head_count, HEAD_DIM)
    value_heads = value_piece.reshape(piece_rows, head_count, HEAD_DIM)
    scores = (
        jnp.einsum("qhd,khd->hqk", query_heads, key_heads, preferred_element_type=jnp.float32)
        * factor
    )
    new_max = jnp.maximum(running_max, jnp.max(scores, axis=2))
    exponent = jnp.exp(scores - new_max[:, :, None])
    running_sum = jnp.sum(exponent, axis=2)
    accum = jnp.einsum(
        "hqk,khd->hqd",
        exponent.astype(jnp.bfloat16),
        value_heads,
        preferred_element_type=jnp.float32,
    )
    return (new_max, running_sum, accum)


def finish(state):
    _, running_sum, accum = state
    result = accum / running_sum[:, :, None]
    return jnp.transpose(result, (1, 0, 2)).reshape(result.shape[1], -1).astype(jnp.bfloat16)


def shift_columns(window, col_shift):
    if col_shift == 0:
        return window
    edge = jnp.zeros(window.shape[:-1] + (1,), window.dtype)
    if col_shift < 0:
        return jnp.concatenate([edge, window[..., :-1]], axis=-1)
    return jnp.concatenate([window[..., 1:], edge], axis=-1)


def tap_sum(running, piece_block, layer_weight):
    piece_rows = piece_block.shape[0]
    frames = piece_block.shape[1]
    band_rows = piece_block.shape[2] - 2
    framed = jnp.pad(piece_block, ((0, 0), (1, 1), (0, 0), (0, 0)))
    for frame_off in range(3):
        for row_off in range(3):
            for col_off in range(3):
                window = shift_columns(
                    framed[:, frame_off : frame_off + frames, row_off : row_off + band_rows, :],
                    col_off - 1,
                )
                tap_weight = layer_weight[frame_off * 9 + row_off * 3 + col_off]
                running = running + lax.dot_general(
                    tap_weight,
                    window.reshape(piece_rows, -1),
                    (((1,), (0,)), ((), ())),
                    preferred_element_type=jnp.float32,
                )
    return running


def make_pick(tile_position, own_rows, piece_block):
    selector = (own_rows[:, None] == tile_position[None, :]).astype(jnp.bfloat16)
    return jnp.einsum("tp,plfc->lftc", selector, piece_block, preferred_element_type=jnp.float32)


def gathered_shards(
    queries,
    key_tokens,
    value_tokens,
    stream,
    norm_gain,
    latent_weight,
    tile_pool,
    tile_position,
    lift_weight,
    lift_bias,
    conv_weight,
):
    query_heads, initial = prepare(queries)
    state = make_update(
        query_heads,
        initial,
        (
            lax.all_gather(key_tokens, ("seq", "rep"), axis=0, tiled=True),
            lax.all_gather(value_tokens, ("seq", "rep"), axis=0, tiled=True),
        ),
    )
    attended = finish(state)
    combined = stream.astype(jnp.float32) + attended.astype(jnp.float32)
    hidden = combined.astype(jnp.bfloat16)
    widened = hidden.astype(jnp.float32)
    scaled = (widened * norm_gain).astype(jnp.bfloat16)
    partial_proj = jnp.dot(scaled, latent_weight, preferred_element_type=jnp.float32)
    partial_squares = jnp.sum(widened * widened, axis=1)
    projected, squares = (
        lax.psum(partial_proj.astype(jnp.bfloat16), "head").astype(jnp.float32),
        lax.psum(partial_squares.astype(jnp.bfloat16), "head").astype(jnp.float32),
    )
    latents = projected * lax.rsqrt(squares / WIDTH + epsilon)[:, None]
    tiles_here = tile_pool.shape[0]
    frames = tile_pool.shape[2]
    columns = tile_pool.shape[3]
    own_rows = lax.axis_index("seq") * tiles_here + jnp.arange(tiles_here, dtype=jnp.int32)
    collected = make_pick(
        tile_position, own_rows, lax.all_gather(tile_pool, "seq", axis=0, tiled=True)
    )
    latent_grid = collected.astype(jnp.bfloat16)
    channels_here = lift_weight.shape[1]
    feature_map = (
        lax.dot_general(
            lift_weight,
            latent_grid.reshape(latent_grid.shape[0], -1),
            (((0,), (0,)), ((), ())),
            preferred_element_type=jnp.float32,
        )
        + lift_bias[:, None]
    )
    for layer_index in range(conv_weight.shape[0]):
        layer_weight = conv_weight[layer_index]
        active = (
            jax.nn.silu(feature_map)
            .astype(jnp.bfloat16)
            .reshape(channels_here, frames, tiles_here, columns)
        )
        zeros_here = jnp.zeros(feature_map.shape, jnp.float32)
        bordered = padded(active, (("seq", 2),), 1)
        rimmed = lax.all_gather(bordered, ("head", "rep"), axis=0, tiled=True)
        update = tap_sum(zeros_here, rimmed, layer_weight)
        feature_map = feature_map + update
    decoded = feature_map.reshape(channels_here, frames, tiles_here, columns)
    return (hidden, latents, decoded)


def fits(queries, tile_pool):
    chips = lax.axis_size("seq")
    heads = queries.shape[1] // HEAD_DIM
    return (
        lax.axis_size("head") == 2
        and lax.axis_size("rep") == 2
        and heads % chips == 0
        and heads // chips % 2 == 0
        and heads >= chips
        and tile_pool.shape[0] == 1
        and tile_pool.shape[2] == 2
        and tile_pool.shape[3] == 128
    )


def whole_vmem(count):
    return [pl.BlockSpec(memory_space=pltpu.VMEM) for _ in range(count)]


def limit(mebibytes):
    return pltpu.CompilerParams(vmem_limit_bytes=mebibytes * 2**20)


def in_hbm(count):
    return [pl.BlockSpec(memory_space=pltpu.HBM) for _ in range(count)]


def kept(array):
    return pltpu.with_memory_space_constraint(array, pltpu.HBM)


def pack(sources, tile, chips, per_chip, first, count):
    rows = sources[0].shape[0]
    tile_rows = 0 if tile is None else tile.shape[1]
    length = 3 * count * rows + tile_rows

    def kernel(*refs):
        inputs, messages = (refs[: len(operands)], refs[len(operands) : -2])
        blocks, sem = refs[-2:]
        here = lax.axis_index("seq")
        copies = []
        for shift in range(chips):
            chip = lax.rem(here + shift, chips)
            column = pl.multiple_of((chip * per_chip + first) * HEAD_DIM, HEAD_DIM)
            for kind in range(3):
                copies.append(
                    pltpu.make_async_copy(
                        inputs[kind].at[:, pl.ds(column, count * HEAD_DIM)],
                        blocks.at[3 * shift + kind],
                        sem.at[3 * shift + kind],
                    )
                )
        order = [3 * shift + kind for shift in list(range(1, chips)) + [0] for kind in range(3)]
        for at in order:
            copies[at].start()
        if tile is not None:
            core = lax.axis_index("rep")
            frames = [inputs[3][0, :, frame, :].astype(jnp.float32) for frame in range(2)]
            half = jnp.where(core == 0, frames[0], frames[1]).astype(jnp.bfloat16)
            for shift in range(chips):
                messages[shift][pl.ds(3 * count * rows, tile_rows), :] = half
        for at in order:
            shift, kind = divmod(at, 3)
            copies[at].wait()
            for head in range(count):
                messages[shift][pl.ds((kind * count + head) * rows, rows), :] = blocks[
                    at, :, pl.ds(head * HEAD_DIM, HEAD_DIM)
                ]

    operands = [kept(source) for source in sources] + ([] if tile is None else [tile])
    return pl.pallas_call(
        kernel,
        out_shape=[pltpu.VMEM((length, HEAD_DIM), jnp.bfloat16)] * chips,
        in_specs=in_hbm(3) + ([] if tile is None else whole_vmem(1)),
        out_specs=whole_vmem(chips),
        scratch_shapes=[
            pltpu.VMEM((3 * chips, rows, count * HEAD_DIM), jnp.bfloat16),
            pltpu.SemaphoreType.DMA((3 * chips,)),
        ],
        compiler_params=limit(12),
    )(*operands)


def join(messages, count, rows, tile_rows):
    pieces = len(messages)

    def kernel(*refs):
        inputs, joined = (refs[:-1], refs[-1])
        for head in range(count):
            for kind in range(2):
                for piece in range(pieces):
                    joined[pl.ds(((2 * head + kind) * pieces + piece) * rows, rows), :] = inputs[piece][
                        pl.ds(((kind + 1) * count + head) * rows, rows), :
                    ]
        if tile_rows:
            for piece in range(pieces):
                joined[pl.ds(2 * count * pieces * rows + piece * tile_rows, tile_rows), :] = inputs[piece][
                    pl.ds(3 * count * rows, tile_rows), :
                ]

    return pl.pallas_call(
        kernel,
        out_shape=jax.ShapeDtypeStruct((pieces * (2 * count * rows + tile_rows), HEAD_DIM), jnp.bfloat16),
        in_specs=whole_vmem(pieces),
        out_specs=pl.BlockSpec(memory_space=pltpu.VMEM),
        compiler_params=limit(8),
    )(*messages)


def attend(messages, own, partner, count, rows):
    pieces = len(messages)
    factor = math.log2(math.e) / math.sqrt(HEAD_DIM)

    def kernel(*refs):
        inputs, (own_ref, partner_ref), outputs = (refs[:pieces], refs[pieces : pieces + 2], refs[pieces + 2 :])
        length = pieces * rows
        for head in range(count):
            query = jnp.concatenate([m[pl.ds(head * rows, rows), :] for m in inputs], axis=0)
            start = 2 * head * length
            key = jnp.concatenate([own_ref[pl.ds(start, length), :], partner_ref[pl.ds(start, length), :]], axis=0)
            start = start + length
            value = jnp.concatenate([own_ref[pl.ds(start, length), :], partner_ref[pl.ds(start, length), :]], axis=0)
            scores = lax.dot_general(query, key, (((1,), (1,)), ((), ())), preferred_element_type=jnp.float32)
            peak = jnp.max(scores, axis=1, keepdims=True)
            exponent = jnp.exp2((scores - peak) * factor)
            total = jnp.sum(exponent, axis=1, keepdims=True)
            summed = jnp.dot(exponent.astype(jnp.bfloat16), value, preferred_element_type=jnp.float32)
            result = (summed / total).astype(jnp.bfloat16)
            for piece in range(pieces):
                outputs[piece][pl.ds(head * rows, rows), :] = result[piece * rows : (piece + 1) * rows, :]

    shape = jax.ShapeDtypeStruct((count * rows, HEAD_DIM), jnp.bfloat16)
    return pl.pallas_call(
        kernel,
        out_shape=[shape] * pieces,
        in_specs=whole_vmem(pieces + 2),
        out_specs=whole_vmem(pieces),
        compiler_params=limit(24),
    )(*messages, own, partner)


def close(chunks, stream, gain, latent_weight, counts, per_chip):
    rows, columns = stream.shape
    latent = latent_weight.shape[0]
    pieces = len(chunks[0])
    flat = [piece for chunk in chunks for piece in chunk]

    def kernel(*refs):
        here = lax.axis_index("seq")
        inputs = refs[: len(flat)]
        stream_ref, gain_ref, weight_ref, hidden_ref, part_ref = refs[len(flat) :]
        projected = jnp.zeros((latent, rows), jnp.float32)
        squares = jnp.zeros((rows, HEAD_DIM), jnp.float32)
        for piece in range(pieces):
            base = pl.multiple_of(
                lax.rem(here + piece, pieces) * (per_chip * HEAD_DIM), per_chip * HEAD_DIM
            )
            span = pl.ds(base, per_chip * HEAD_DIM)
            blocks = []
            for index, count in enumerate(counts):
                source = inputs[index * pieces + piece]
                blocks.extend(source[pl.ds(head * rows, rows), :] for head in range(count))
            attended = jnp.concatenate(blocks, axis=1)
            hidden = (stream_ref[:, span].astype(jnp.float32) + attended.astype(jnp.float32)).astype(jnp.bfloat16)
            hidden_ref[:, span] = hidden
            widened = hidden.astype(jnp.float32)
            scaled = (widened * gain_ref[:, span]).astype(jnp.bfloat16)
            projected = projected + lax.dot_general(
                weight_ref[:, span], scaled, (((1,), (1,)), ((), ())), preferred_element_type=jnp.float32
            )
            squared = widened * widened
            for head in range(per_chip):
                squares = squares + squared[:, head * HEAD_DIM : (head + 1) * HEAD_DIM]
        total = jnp.sum(squares.T, axis=0, keepdims=True)
        part_ref[pl.ds(0, latent), :] = projected
        part_ref[pl.ds(latent, 8), :] = jnp.broadcast_to(total, (8, rows))

    return pl.pallas_call(
        kernel,
        out_shape=[
            jax.ShapeDtypeStruct((rows, columns), jnp.bfloat16),
            jax.ShapeDtypeStruct((latent + 8, rows), jnp.float32),
        ],
        in_specs=whole_vmem(len(flat) + 3),
        out_specs=whole_vmem(2),
        compiler_params=limit(12),
        name="close",
    )(*flat, stream, gain, latent_weight)


def silu(value):
    return value / (1.0 + jnp.exp(-value))


def store_shifted(windows, block, active):
    depth, columns = active.shape
    lane = lax.broadcasted_iota(jnp.int32, (depth, columns), 1)
    before = jnp.where(lane == 0, 0.0, pltpu.roll(active, 1, 1))
    after = jnp.where(lane == columns - 1, 0.0, pltpu.roll(active, columns - 1, 1))
    for tap, window in enumerate((before, active, after)):
        windows[pl.ds(tap * depth, depth), pl.ds(block * columns, columns)] = window.astype(jnp.bfloat16)


def frame_taps(weights, windows, frame_tap, width, in_rows, out_rows, totals):
    for row_tap in range(3):
        first = 9 * frame_tap + 3 * row_tap
        taps = jnp.concatenate([weights[first + tap] for tap in range(3)], axis=1)
        for frame in range(2):
            source = frame + frame_tap - 1
            if 0 <= source < 2:
                window = windows[:, pl.ds((source * in_rows + row_tap) * width, out_rows * width)]
                totals[frame] = totals[frame] + jnp.dot(taps, window, preferred_element_type=jnp.float32)
    return totals


def first_layer(position, own_tiles, partner_tiles, lift_all, lift_own, conv_weight):
    chips = position.shape[0]
    latent = own_tiles.shape[0] // chips
    width = own_tiles.shape[1]
    channels, own_channels = (lift_all.shape[0], lift_own.shape[0])
    taps = conv_weight.shape[1]

    def kernel(
        position_ref, own_ref, partner_ref, all_ref, mine_ref, weight_ref, active_ref, feature_ref,
        weights, windows, sem,
    ):
        third = taps // 3
        copies = [
            pltpu.make_async_copy(
                weight_ref.at[0, pl.ds(part * third, third)], weights.at[pl.ds(part * third, third)], sem.at[part]
            )
            for part in range(3)
        ]
        for copy in copies:
            copy.start()
        row, core = (lax.axis_index("seq"), lax.axis_index("rep"))

        def tile_of(source, target):
            picked = jnp.zeros((latent, width), jnp.float32)
            for piece in range(chips):
                tile = source[pl.ds(piece * latent, latent), :].astype(jnp.float32)
                named = position_ref[lax.rem(row + chips - piece, chips)]
                picked = jnp.where(named == target, tile, picked)
            return picked

        weight_all = all_ref[:, :latent].astype(jnp.bfloat16)
        bias_all = all_ref[:, latent : latent + 1]
        grid = [[None] * 5, [None] * 5]
        for offset in range(5):
            target = row + offset - 2
            inside = jnp.logical_and(target >= 0, target < chips)
            mine, other = (tile_of(own_ref, target), tile_of(partner_ref, target))
            grid[0][offset] = jnp.where(core == 0, mine, other).astype(jnp.bfloat16)
            grid[1][offset] = jnp.where(core == 0, other, mine).astype(jnp.bfloat16)
            for frame in range(2):
                lifted = (
                    jnp.dot(weight_all, grid[frame][offset], preferred_element_type=jnp.float32) + bias_all
                )
                active = jnp.where(inside, silu(lifted), 0.0)
                store_shifted(windows, frame * 5 + offset, active)
        weight_own = mine_ref[:, :latent].astype(jnp.bfloat16)
        bias_own = mine_ref[:, latent : latent + 1]
        totals = [jnp.zeros((own_channels, 3 * width), jnp.float32) for _ in range(2)]
        for frame_tap in range(3):
            copies[frame_tap].wait()
            totals = frame_taps(weights, windows, frame_tap, width, 5, 3, totals)
        for frame in range(2):
            near = jnp.concatenate(grid[frame][1:4], axis=1)
            feature = (
                jnp.dot(weight_own, near, preferred_element_type=jnp.float32) + bias_own
            ) + totals[frame]
            feature_ref[:, pl.ds(frame * width, width)] = feature[:, width : 2 * width]
            for offset in range(3):
                target = row + offset - 1
                inside = jnp.logical_and(target >= 0, target < chips)
                block = silu(feature[:, offset * width : (offset + 1) * width])
                active_ref[:, pl.ds((frame * 3 + offset) * width, width)] = jnp.where(
                    inside, block, 0.0
                ).astype(jnp.bfloat16)

    return pl.pallas_call(
        kernel,
        out_shape=[
            jax.ShapeDtypeStruct((own_channels, 6 * width), jnp.bfloat16),
            jax.ShapeDtypeStruct((own_channels, 2 * width), jnp.float32),
        ],
        in_specs=[pl.BlockSpec(memory_space=pltpu.SMEM)] + whole_vmem(4) + in_hbm(1),
        out_specs=whole_vmem(2),
        scratch_shapes=[
            pltpu.VMEM((taps, own_channels, channels), jnp.bfloat16),
            pltpu.VMEM((3 * channels, 10 * width), jnp.bfloat16),
            pltpu.SemaphoreType.DMA((3,)),
        ],
        compiler_params=limit(24),
        name="first_layer",
    )(position, own_tiles, partner_tiles, lift_all, lift_own, kept(conv_weight))


def second_layer(active, feature, conv_weight):
    channels = active.shape[0]
    width = active.shape[1] // 6
    own_channels = feature.shape[0]
    taps = conv_weight.shape[1]

    def kernel(active_ref, feature_ref, weight_ref, decoded_ref, weights, windows, sem):
        third = taps // 3
        copies = [
            pltpu.make_async_copy(
                weight_ref.at[1, pl.ds(part * third, third)], weights.at[pl.ds(part * third, third)], sem.at[part]
            )
            for part in range(3)
        ]
        for copy in copies:
            copy.start()
        for block in range(6):
            store_shifted(windows, block, active_ref[:, pl.ds(block * width, width)].astype(jnp.float32))
        totals = [jnp.zeros((own_channels, width), jnp.float32) for _ in range(2)]
        for frame_tap in range(3):
            copies[frame_tap].wait()
            totals = frame_taps(weights, windows, frame_tap, width, 3, 1, totals)
        for frame in range(2):
            decoded_ref[:, frame, :] = feature_ref[:, pl.ds(frame * width, width)] + totals[frame]

    return pl.pallas_call(
        kernel,
        out_shape=jax.ShapeDtypeStruct((own_channels, 2, width), jnp.float32),
        in_specs=whole_vmem(2) + in_hbm(1),
        out_specs=pl.BlockSpec(memory_space=pltpu.VMEM),
        scratch_shapes=[
            pltpu.VMEM((taps, own_channels, channels), jnp.bfloat16),
            pltpu.VMEM((3 * channels, 6 * width), jnp.bfloat16),
            pltpu.SemaphoreType.DMA((3,)),
        ],
        compiler_params=limit(16),
        name="second_layer",
    )(active, feature, kept(conv_weight))


def exchanged_shards(
    queries,
    key_tokens,
    value_tokens,
    stream,
    norm_gain,
    latent_weight,
    tile_pool,
    tile_position,
    lift_weight,
    lift_bias,
    conv_weight,
):
    chips = lax.axis_size("seq")
    rows = queries.shape[0]
    per_chip = queries.shape[1] // HEAD_DIM // chips
    count = per_chip // 2
    latent_channels = tile_pool.shape[1]
    onward = [[(i, (i + shift) % chips) for i in range(chips)] for shift in range(chips)]
    back = [[(j, i) for i, j in pairs] for pairs in onward]
    swap = [(0, 1), (1, 0)]
    sources = (queries, key_tokens, value_tokens)

    def send(messages):
        arrived = [messages[0]]
        for shift in range(1, chips):
            arrived.append(lax.ppermute(messages[shift], "seq", onward[shift]))
        return arrived

    def give_back(results):
        home = [results[0]]
        for shift in range(1, chips):
            home.append(lax.ppermute(results[shift], "seq", back[shift]))
        return home

    early = pack(sources, tile_pool, chips, per_chip, 0, count)
    late = pack(sources, None, chips, per_chip, count, count)
    early_in, late_in = (send(early), send(late))

    lift_weight, lift_bias, _ = lax.optimization_barrier((lift_weight, lift_bias, late[0]))
    lift_own = jnp.concatenate(
        [
            lift_weight.T.astype(jnp.float32),
            lift_bias[:, None],
            jnp.zeros((lift_bias.shape[0], 128 - latent_channels - 1), jnp.float32),
        ],
        axis=1,
    )
    lift_all = lax.all_gather(lift_own, ("head", "rep"), axis=0, tiled=True)

    early_in, lift_all = lax.optimization_barrier((early_in, lift_all))
    own = join(early_in, count, rows, latent_channels)
    partner = lax.ppermute(own, "rep", swap)
    tiles_at = 2 * count * chips * rows
    early_out = attend(early_in, own, partner, count, rows)
    early_home = give_back(early_out)

    own, partner, _ = lax.optimization_barrier((own, partner, early_out[0]))
    active, feature = first_layer(tile_position, own[tiles_at:], partner[tiles_at:], lift_all, lift_own, conv_weight)
    active_all = lax.all_gather(active, ("head", "rep"), axis=0, tiled=True)

    late_in, active_all = lax.optimization_barrier((late_in, active_all))
    own = join(late_in, count, rows, 0)
    partner = lax.ppermute(own, "rep", swap)
    late_out = attend(late_in, own, partner, count, rows)
    late_home = give_back(late_out)

    active_all, _ = lax.optimization_barrier((active_all, late_out[0]))
    decoded = second_layer(active_all, feature, conv_weight)
    decoded = decoded[:, :, None, :]

    hidden, part = close(
        (early_home, late_home), stream, norm_gain[None, :], latent_weight.T, (count, count), per_chip
    )
    part = part + lax.ppermute(part, "head", swap)
    latent = latent_weight.shape[1]
    latents = part[:latent] * lax.rsqrt(part[latent : latent + 1] / WIDTH + epsilon)
    return (hidden, latents.T, decoded)


def shards(*arrays):
    form = exchanged_shards if fits(arrays[0], arrays[6]) else gathered_shards
    return form(*arrays)


def solution(mesh):
    in_specs = (
        P(("groups", "seq", "rep"), "head"),
        P(("groups", "seq", "rep"), "head"),
        P(("groups", "seq", "rep"), "head"),
        P(("groups", "seq", "rep"), "head"),
        P("head"),
        P("head", None),
        P(("groups", "seq"), None, None, None),
        P("groups"),
        P(None, ("head", "rep")),
        P(("head", "rep")),
        P(None, None, ("head", "rep"), None),
    )
    out_specs = (
        P(("groups", "seq", "rep"), "head"),
        P(("groups", "seq", "rep"), None),
        P(("groups", "head", "rep"), None, "seq", None),
    )
    return jax.shard_map(shards, mesh=mesh, in_specs=in_specs, out_specs=out_specs, check_vma=False)
```

profile of v0, /device:TPU:0, one launch (start us, length us, event | category | flops | bytes accessed | tf_op | source)
XLA Modules:
  0.0 91.5 jit_solution(565298723324918090)
XLA Ops:
  0.6 0.7 copy-done.2
  1.4 1.5 %shard_map.130 = (bf16[1216,128]{1,0:T(8,128)(2,1)S(1)}, bf16[1216,128]{1,0:T(8,128)(2,1)S(1)}, bf16[1216,128]{1,0:T(8,128)(2,1)S(1)}, bf16[1216,128]{1,0:T(8,128)(2,1)S(1)}) custom-call(bf16[128,3072]{1,0:T(8,128)(2,1)} %refs_0_.3, bf16[128,3072]{1,0:T(8,128)(2,1)} %refs_1_.3, bf16[128,3072]{1,0:T(8,128)(2,1)} %refs_2_.3, bf16[1,64,2,128]{3,2,1,0:T(2,128)(2,1)S(1)} %copy-done.2), custom_call_target="tpu_custom_call" | custom-call | tf_op jit(solution)/shard_map/pallas_call | solution.py:247
  2.9 3.1 %collective-permute-start = (bf16[1216,128]{1,0:T(8,128)(2,1)S(1)}, bf16[1216,128]{1,0:T(8,128)(2,1)S(1)}, u32[]{:S(2)}, u32[]{:S(2)}) collective-permute-start(bf16[1216,128]{1,0:T(8,128)(2,1)S(1)} %get-tuple-element.39), channel_id=1, source_target_pairs={{0,4},{4,8},{8,12},{12,0},{1,5},{5,9},{9,13},{13,1},{2,6},{6,10},{... | collective-permute-start | bytes 933896 | tf_op jit(solution)/shard_map/ppermute | solution.py:541
  6.0 2.6 %collective-permute-start.1 = (bf16[1216,128]{1,0:T(8,128)(2,1)S(1)}, bf16[1216,128]{1,0:T(8,128)(2,1)S(1)}, u32[]{:S(2)}, u32[]{:S(2)}) collective-permute-start(bf16[1216,128]{1,0:T(8,128)(2,1)S(1)} %get-tuple-element.40), channel_id=1, source_target_pairs={{0,8},{4,12},{8,0},{12,4},{1,9},{5,13},{9,1},{13,5},{2,10},{6,14},... | collective-permute-start | bytes 933896 | tf_op jit(solution)/shard_map/ppermute | solution.py:541
  8.6 1.3 %collective-permute-start.2 = (bf16[1216,128]{1,0:T(8,128)(2,1)S(1)}, bf16[1216,128]{1,0:T(8,128)(2,1)S(1)}, u32[]{:S(2)}, u32[]{:S(2)}) collective-permute-start(bf16[1216,128]{1,0:T(8,128)(2,1)S(1)} %get-tuple-element.41), channel_id=1, source_target_pairs={{0,12},{4,0},{8,4},{12,8},{1,13},{5,1},{9,5},{13,9},{2,14},{6,2},{... | collective-permute-start | bytes 933896 | tf_op jit(solution)/shard_map/ppermute | solution.py:541
  9.9 1.5 %shard_map.131 = (bf16[1152,128]{1,0:T(8,128)(2,1)S(1)}, bf16[1152,128]{1,0:T(8,128)(2,1)S(1)}, bf16[1152,128]{1,0:T(8,128)(2,1)S(1)}, bf16[1152,128]{1,0:T(8,128)(2,1)S(1)}) custom-call(bf16[128,3072]{1,0:T(8,128)(2,1)} %refs_0_.3, bf16[128,3072]{1,0:T(8,128)(2,1)} %refs_1_.3, bf16[128,3072]{1,0:T(8,128)(2,1)} %refs_2_.3), custom_call_target="tpu_custom_call" | custom-call | tf_op jit(solution)/shard_map/pallas_call | solution.py:247
  11.4 0.8 copy.18
  12.2 0.8 copy.17
  13.0 0.1 pad.2.clone
  13.1 0.1 maximum_maximum_fusion.mine_ref
  13.1 5.8 %all_gather.6.all_ref = f32[512,128]{1,0:T(8,128)S(1)} all-gather(f32[128,128]{1,0:T(8,128)S(1)} %maximum_maximum_fusion.mine_ref), channel_id=1, replica_groups=mesh['groups'=2,'seq'=4,'head'=2,'rep'=2] {'head','rep'}, dimensions={0}, use_global_device_ids=true | all-gather | bytes 327680 | tf_op jit(solution)/shard_map/all_gather | solution.py:563
  18.9 9.9 %collective-permute-done.1.refs_2_ = bf16[1216,128]{1,0:T(8,128)(2,1)S(1)} collective-permute-done((bf16[1216,128]{1,0:T(8,128)(2,1)S(1)}, bf16[1216,128]{1,0:T(8,128)(2,1)S(1)}, u32[]{:S(2)}, u32[]{:S(2)}) %collective-permute-start.1) | collective-permute-done | bytes 311328 | tf_op jit(solution)/shard_map/ppermute | solution.py:541
  28.9 0.1 collective-permute-start.3
  29.0 7.2 %collective-permute-start.7 = (bf16[1152,128]{1,0:T(8,128)(2,1)S(1)}, bf16[1152,128]{1,0:T(8,128)(2,1)S(1)}, u32[]{:S(2)}, u32[]{:S(2)}) collective-permute-start(bf16[1152,128]{1,0:T(8,128)(2,1)S(1)} %get-tuple-element.53), channel_id=1, source_target_pairs={{0,4},{4,8},{8,12},{12,0},{1,5},{5,9},{9,13},{13,1},{2,6},{6,10},{... | collective-permute-start | bytes 884744 | tf_op jit(solution)/shard_map/ppermute | solution.py:541
  36.2 1.6 %collective-permute-start.8 = (bf16[1152,128]{1,0:T(8,128)(2,1)S(1)}, bf16[1152,128]{1,0:T(8,128)(2,1)S(1)}, u32[]{:S(2)}, u32[]{:S(2)}) collective-permute-start(bf16[1152,128]{1,0:T(8,128)(2,1)S(1)} %get-tuple-element.54), channel_id=1, source_target_pairs={{0,8},{4,12},{8,0},{12,4},{1,9},{5,13},{9,1},{13,5},{2,10},{6,14},... | collective-permute-start | bytes 884744 | tf_op jit(solution)/shard_map/ppermute | solution.py:541
  37.8 0.9 collective-permute-start.9
  38.6 2.7 %shard_map.133 = (bf16[384,128]{1,0:T(8,128)(2,1)S(1)}, bf16[384,128]{1,0:T(8,128)(2,1)S(1)}, bf16[384,128]{1,0:T(8,128)(2,1)S(1)}, bf16[384,128]{1,0:T(8,128)(2,1)S(1)}) custom-call(bf16[1216,128]{1,0:T(8,128)(2,1)S(1)} %get-tuple-element.45.refs_0_, bf16[1216,128]{1,0:T(8,128)(2,1)S(1)} %collective-permute-done.refs_1_, ...), custom_call_target="tpu_custom_call" | custom-call | tf_op jit(solution)/shard_map/pallas_call | solution.py:309
  41.4 5.7 %first_layer.1 = (bf16[128,768]{1,0:T(8,128)(2,1)S(1)}, f32[128,256]{1,0:T(8,128)S(1)}) custom-call(s32[4]{0:T(128)S(1)} %copy-done.4, bf16[256,128]{1,0:T(8,128)(2,1)S(1)} %slice.12.own_ref, bf16[256,128]{1,0:T(8,128)(2,1)S(1)} %slice.13.partner_ref, f32[512,128]{1,0:T(8,128)S(1)} %all_gather.6.all_ref, f32[128,128]{1,0:T(8,128)S(1)} %maximum_maximum_fusion.mine_ref, ...), custom_call_target="tpu_custom_call" | custom-call | tf_op jit(solution)/shard_map/first_layer/pallas_call | solution.py:457
  47.1 8.6 %all_gather.7.active_ref = bf16[512,768]{1,0:T(8,128)(2,1)S(1)} all-gather(bf16[128,768]{1,0:T(8,128)(2,1)S(1)} %get-tuple-element.59), channel_id=1, replica_groups=mesh['groups'=2,'seq'=4,'head'=2,'rep'=2] {'head','rep'}, dimensions={0}, use_global_device_ids=true | all-gather | bytes 983040 | tf_op jit(solution)/shard_map/all_gather | solution.py:574
  55.7 1.9 %collective-permute-done.8.refs_2_ = bf16[1152,128]{1,0:T(8,128)(2,1)S(1)} collective-permute-done((bf16[1152,128]{1,0:T(8,128)(2,1)S(1)}, bf16[1152,128]{1,0:T(8,128)(2,1)S(1)}, u32[]{:S(2)}, u32[]{:S(2)}) %collective-permute-start.8) | collective-permute-done | bytes 294944 | tf_op jit(solution)/shard_map/ppermute | solution.py:541
  57.7 7.6 %collective-permute-start.4 = (bf16[384,128]{1,0:T(8,128)(2,1)S(1)}, bf16[384,128]{1,0:T(8,128)(2,1)S(1)}, u32[]{:S(2)}, u32[]{:S(2)}) collective-permute-start(bf16[384,128]{1,0:T(8,128)(2,1)S(1)} %get-tuple-element.50), channel_id=1, source_target_pairs={{4,0},{8,4},{12,8},{0,12},{5,1},{9,5},{13,9},{1,13},{6,2},{10,6},{... | collective-permute-start | bytes 294920 | tf_op jit(solution)/shard_map/ppermute | solution.py:547
  65.3 0.7 collective-permute-start.5
  66.0 2.6 %shard_map.135 = (bf16[384,128]{1,0:T(8,128)(2,1)S(1)}, bf16[384,128]{1,0:T(8,128)(2,1)S(1)}, bf16[384,128]{1,0:T(8,128)(2,1)S(1)}, bf16[384,128]{1,0:T(8,128)(2,1)S(1)}) custom-call(bf16[1152,128]{1,0:T(8,128)(2,1)S(1)} %get-tuple-element.60.refs_0_, bf16[1152,128]{1,0:T(8,128)(2,1)S(1)} %collective-permute-done.7.refs_1_, ...), custom_call_target="tpu_custom_call" | custom-call | tf_op jit(solution)/shard_map/pallas_call | solution.py:309
  68.7 3.9 %collective-permute-start.11 = (bf16[384,128]{1,0:T(8,128)(2,1)S(1)}, bf16[384,128]{1,0:T(8,128)(2,1)S(1)}, u32[]{:S(2)}, u32[]{:S(2)}) collective-permute-start(bf16[384,128]{1,0:T(8,128)(2,1)S(1)} %get-tuple-element.65), channel_id=1, source_target_pairs={{4,0},{8,4},{12,8},{0,12},{5,1},{9,5},{13,9},{1,13},{6,2},{10,6},{... | collective-permute-start | bytes 294920 | tf_op jit(solution)/shard_map/ppermute | solution.py:547
  72.6 0.4 collective-permute-start.12
  73.0 1.4 %collective-permute-start.13 = (bf16[384,128]{1,0:T(8,128)(2,1)S(1)}, bf16[384,128]{1,0:T(8,128)(2,1)S(1)}, u32[]{:S(2)}, u32[]{:S(2)}) collective-permute-start(bf16[384,128]{1,0:T(8,128)(2,1)S(1)} %get-tuple-element.67), channel_id=1, source_target_pairs={{12,0},{0,4},{4,8},{8,12},{13,1},{1,5},{5,9},{9,13},{14,2},{2,6},{... | collective-permute-start | bytes 294920 | tf_op jit(solution)/shard_map/ppermute | solution.py:547
  74.4 5.8 %collective-permute-done.5.refs_2_ = bf16[384,128]{1,0:T(8,128)(2,1)S(1)} collective-permute-done((bf16[384,128]{1,0:T(8,128)(2,1)S(1)}, bf16[384,128]{1,0:T(8,128)(2,1)S(1)}, u32[]{:S(2)}, u32[]{:S(2)}) %collective-permute-start.5) | collective-permute-done | bytes 98336 | tf_op jit(solution)/shard_map/ppermute | solution.py:547
  80.1 3.8 %collective-permute-done.12.refs_6_ = bf16[384,128]{1,0:T(8,128)(2,1)S(1)} collective-permute-done((bf16[384,128]{1,0:T(8,128)(2,1)S(1)}, bf16[384,128]{1,0:T(8,128)(2,1)S(1)}, u32[]{:S(2)}, u32[]{:S(2)}) %collective-permute-start.12) | collective-permute-done | bytes 98336 | tf_op jit(solution)/shard_map/ppermute | solution.py:547
  83.9 1.3 %close.1 = (bf16[128,3072]{1,0:T(8,128)(2,1)}, f32[72,128]{1,0:T(8,128)S(1)}) custom-call(bf16[384,128]{1,0:T(8,128)(2,1)S(1)} %get-tuple-element.49.refs_0_, bf16[384,128]{1,0:T(8,128)(2,1)S(1)} %collective-permute-done.4.refs_1_, bf16[384,128]{1,0:T(8,128)(2,1)S(1)} %collective-permute-done.5.refs_2_, bf16[384,128]{1,0:T(8,128)(2,1)S(1)} %collective-permute-done.6.refs_3_, ...), custom_call_target="tpu_custom_call" | custom-call | tf_op jit(solution)/shard_map/close/pallas_call | solution.py:354
  85.3 1.5 %collective-permute-start.14 = (f32[72,128]{1,0:T(8,128)S(1)}, f32[72,128]{1,0:T(8,128)S(1)}, u32[]{:S(2)}, u32[]{:S(2)}) collective-permute-start(f32[72,128]{1,0:T(8,128)S(1)} %get-tuple-element.69), channel_id=1, source_target_pairs={{0,2},{2,0},{1,3},{3,1},{4,6},{6,4},{5,7},{7,5},{8,10},{10,8},{9,1... | collective-permute-start | bytes 110600 | tf_op jit(solution)/shard_map/ppermute | solution.py:589
  86.7 4.1 %second_layer.1 = f32[128,2,128]{2,1,0:T(2,128)} custom-call(bf16[512,768]{1,0:T(8,128)(2,1)S(1)} %all_gather.7.active_ref, f32[128,256]{1,0:T(8,128)S(1)} %get-tuple-element.72.feature_ref, bf16[2,27,128,512]{3,2,1,0:T(8,128)(2,1)} %weight_ref.3), custom_call_target="tpu_custom_call" | custom-call | tf_op jit(solution)/shard_map/second_layer/pallas_call | solution.py:500
  90.8 0.6 fusion
  (29 shorter events, 0.3 us)
Async XLA Ops:
  0.6 0.8 copy-start.2
  1.4 40.0 %copy-start.4 = (s32[4]{0:T(128)S(1)}, s32[4]{0:T(128)}, u32[]{:S(2)}) copy-start(s32[4]{0:T(128)} %position_ref.1) | copy-start | bytes 52
  2.9 16.0 %collective-permute-start = (bf16[1216,128]{1,0:T(8,128)(2,1)S(1)}, bf16[1216,128]{1,0:T(8,128)(2,1)S(1)}, u32[]{:S(2)}, u32[]{:S(2)}) collective-permute-start(bf16[1216,128]{1,0:T(8,128)(2,1)S(1)} %get-tuple-element.39), channel_id=1, source_target_pairs={{0,4},{4,8},{8,12},{12,0},{1,5},{5,9},{9,13},{13,1},{2,6},{6,10},{... | collective-permute-start | bytes 933896 | tf_op jit(solution)/shard_map/ppermute | solution.py:541
  6.0 22.9 %collective-permute-start.1 = (bf16[1216,128]{1,0:T(8,128)(2,1)S(1)}, bf16[1216,128]{1,0:T(8,128)(2,1)S(1)}, u32[]{:S(2)}, u32[]{:S(2)}) collective-permute-start(bf16[1216,128]{1,0:T(8,128)(2,1)S(1)} %get-tuple-element.40), channel_id=1, source_target_pairs={{0,8},{4,12},{8,0},{12,4},{1,9},{5,13},{9,1},{13,5},{2,10},{6,14},... | collective-permute-start | bytes 933896 | tf_op jit(solution)/shard_map/ppermute | solution.py:541
  8.6 20.3 %collective-permute-start.2 = (bf16[1216,128]{1,0:T(8,128)(2,1)S(1)}, bf16[1216,128]{1,0:T(8,128)(2,1)S(1)}, u32[]{:S(2)}, u32[]{:S(2)}) collective-permute-start(bf16[1216,128]{1,0:T(8,128)(2,1)S(1)} %get-tuple-element.41), channel_id=1, source_target_pairs={{0,12},{4,0},{8,4},{12,8},{1,13},{5,1},{9,5},{13,9},{2,14},{6,2},{... | collective-permute-start | bytes 933896 | tf_op jit(solution)/shard_map/ppermute | solution.py:541
  28.9 9.7 %collective-permute-start.3 = (bf16[3328,128]{1,0:T(8,128)(2,1)S(1)}, bf16[3328,128]{1,0:T(8,128)(2,1)S(1)}, u32[]{:S(2)}, u32[]{:S(2)}) collective-permute-start(bf16[3328,128]{1,0:T(8,128)(2,1)S(1)} %shard_map.132.refs_4_), channel_id=1, source_target_pairs={{0,1},{1,0},{2,3},{3,2},{4,5},{5,4},{6,7},{7,6},{8,9},{9,8},{10,11... | collective-permute-start | bytes 2555912 | tf_op jit(solution)/shard_map/ppermute | solution.py:567
  29.0 26.7 %collective-permute-start.7 = (bf16[1152,128]{1,0:T(8,128)(2,1)S(1)}, bf16[1152,128]{1,0:T(8,128)(2,1)S(1)}, u32[]{:S(2)}, u32[]{:S(2)}) collective-permute-start(bf16[1152,128]{1,0:T(8,128)(2,1)S(1)} %get-tuple-element.53), channel_id=1, source_target_pairs={{0,4},{4,8},{8,12},{12,0},{1,5},{5,9},{9,13},{13,1},{2,6},{6,10},{... | collective-permute-start | bytes 884744 | tf_op jit(solution)/shard_map/ppermute | solution.py:541
  36.2 21.4 %collective-permute-start.8 = (bf16[1152,128]{1,0:T(8,128)(2,1)S(1)}, bf16[1152,128]{1,0:T(8,128)(2,1)S(1)}, u32[]{:S(2)}, u32[]{:S(2)}) collective-permute-start(bf16[1152,128]{1,0:T(8,128)(2,1)S(1)} %get-tuple-element.54), channel_id=1, source_target_pairs={{0,8},{4,12},{8,0},{12,4},{1,9},{5,13},{9,1},{13,5},{2,10},{6,14},... | collective-permute-start | bytes 884744 | tf_op jit(solution)/shard_map/ppermute | solution.py:541
  37.8 19.8 %collective-permute-start.9 = (bf16[1152,128]{1,0:T(8,128)(2,1)S(1)}, bf16[1152,128]{1,0:T(8,128)(2,1)S(1)}, u32[]{:S(2)}, u32[]{:S(2)}) collective-permute-start(bf16[1152,128]{1,0:T(8,128)(2,1)S(1)} %get-tuple-element.55), channel_id=1, source_target_pairs={{0,12},{4,0},{8,4},{12,8},{1,13},{5,1},{9,5},{13,9},{2,14},{6,2},{... | collective-permute-start | bytes 884744 | tf_op jit(solution)/shard_map/ppermute | solution.py:541
  41.3 42.6 %copy-start = (bf16[128,3072]{1,0:T(8,128)(2,1)S(1)}, bf16[128,3072]{1,0:T(8,128)(2,1)}, u32[]{:S(2)}) copy-start(bf16[128,3072]{1,0:T(8,128)(2,1)} %refs_8_.1) | copy-start | bytes 2359300
  41.3 42.6 %copy-start.1 = (bf16[3072,64]{0,1:T(8,128)(2,1)S(1)}, bf16[3072,64]{0,1:T(8,128)(2,1)}, u32[]{:S(2)}) copy-start(bf16[3072,64]{0,1:T(8,128)(2,1)} %param.16) | copy-start | bytes 1179652
  41.3 42.6 %copy-start.3 = (f32[3072]{0:T(1024)S(1)}, f32[3072]{0:T(1024)}, u32[]{:S(2)}) copy-start(f32[3072]{0:T(1024)} %param.15) | copy-start | bytes 36868
  57.6 8.4 %collective-permute-start.10 = (bf16[3072,128]{1,0:T(8,128)(2,1)S(1)}, bf16[3072,128]{1,0:T(8,128)(2,1)S(1)}, u32[]{:S(2)}, u32[]{:S(2)}) collective-permute-start(bf16[3072,128]{1,0:T(8,128)(2,1)S(1)} %shard_map.134.refs_4_), channel_id=1, source_target_pairs={{0,1},{1,0},{2,3},{3,2},{4,5},{5,4},{6,7},{7,6},{8,9},{9,8},{10,11... | collective-permute-start | bytes 2359304 | tf_op jit(solution)/shard_map/ppermute | solution.py:578
  57.7 15.3 %collective-permute-start.4 = (bf16[384,128]{1,0:T(8,128)(2,1)S(1)}, bf16[384,128]{1,0:T(8,128)(2,1)S(1)}, u32[]{:S(2)}, u32[]{:S(2)}) collective-permute-start(bf16[384,128]{1,0:T(8,128)(2,1)S(1)} %get-tuple-element.50), channel_id=1, source_target_pairs={{4,0},{8,4},{12,8},{0,12},{5,1},{9,5},{13,9},{1,13},{6,2},{10,6},{... | collective-permute-start | bytes 294920 | tf_op jit(solution)/shard_map/ppermute | solution.py:547
  65.3 14.8 %collective-permute-start.5 = (bf16[384,128]{1,0:T(8,128)(2,1)S(1)}, bf16[384,128]{1,0:T(8,128)(2,1)S(1)}, u32[]{:S(2)}, u32[]{:S(2)}) collective-permute-start(bf16[384,128]{1,0:T(8,128)(2,1)S(1)} %get-tuple-element.51), channel_id=1, source_target_pairs={{8,0},{12,4},{0,8},{4,12},{9,1},{13,5},{1,9},{5,13},{10,2},{14,6},... | collective-permute-start | bytes 294920 | tf_op jit(solution)/shard_map/ppermute | solution.py:547
  66.0 14.1 %collective-permute-start.6 = (bf16[384,128]{1,0:T(8,128)(2,1)S(1)}, bf16[384,128]{1,0:T(8,128)(2,1)S(1)}, u32[]{:S(2)}, u32[]{:S(2)}) collective-permute-start(bf16[384,128]{1,0:T(8,128)(2,1)S(1)} %get-tuple-element.52), channel_id=1, source_target_pairs={{12,0},{0,4},{4,8},{8,12},{13,1},{1,5},{5,9},{9,13},{14,2},{2,6},{... | collective-permute-start | bytes 294920 | tf_op jit(solution)/shard_map/ppermute | solution.py:547
  68.7 11.4 %collective-permute-start.11 = (bf16[384,128]{1,0:T(8,128)(2,1)S(1)}, bf16[384,128]{1,0:T(8,128)(2,1)S(1)}, u32[]{:S(2)}, u32[]{:S(2)}) collective-permute-start(bf16[384,128]{1,0:T(8,128)(2,1)S(1)} %get-tuple-element.65), channel_id=1, source_target_pairs={{4,0},{8,4},{12,8},{0,12},{5,1},{9,5},{13,9},{1,13},{6,2},{10,6},{... | collective-permute-start | bytes 294920 | tf_op jit(solution)/shard_map/ppermute | solution.py:547
  72.6 11.3 %collective-permute-start.12 = (bf16[384,128]{1,0:T(8,128)(2,1)S(1)}, bf16[384,128]{1,0:T(8,128)(2,1)S(1)}, u32[]{:S(2)}, u32[]{:S(2)}) collective-permute-start(bf16[384,128]{1,0:T(8,128)(2,1)S(1)} %get-tuple-element.66), channel_id=1, source_target_pairs={{8,0},{12,4},{0,8},{4,12},{9,1},{13,5},{1,9},{5,13},{10,2},{14,6},... | collective-permute-start | bytes 294920 | tf_op jit(solution)/shard_map/ppermute | solution.py:547
  73.0 10.9 %collective-permute-start.13 = (bf16[384,128]{1,0:T(8,128)(2,1)S(1)}, bf16[384,128]{1,0:T(8,128)(2,1)S(1)}, u32[]{:S(2)}, u32[]{:S(2)}) collective-permute-start(bf16[384,128]{1,0:T(8,128)(2,1)S(1)} %get-tuple-element.67), channel_id=1, source_target_pairs={{12,0},{0,4},{4,8},{8,12},{13,1},{1,5},{5,9},{9,13},{14,2},{2,6},{... | collective-permute-start | bytes 294920 | tf_op jit(solution)/shard_map/ppermute | solution.py:547
  85.3 5.6 %collective-permute-start.14 = (f32[72,128]{1,0:T(8,128)S(1)}, f32[72,128]{1,0:T(8,128)S(1)}, u32[]{:S(2)}, u32[]{:S(2)}) collective-permute-start(f32[72,128]{1,0:T(8,128)S(1)} %get-tuple-element.69), channel_id=1, source_target_pairs={{0,2},{2,0},{1,3},{3,1},{4,6},{6,4},{5,7},{7,5},{8,10},{10,8},{9,1... | collective-permute-start | bytes 110600 | tf_op jit(solution)/shard_map/ppermute | solution.py:589
where the time goes:
time: 91.9 us; the launch traced here: 91.5 us
  starting transfers between devices  32.3 us (35%)
  waiting for transfers between devices  21.3 us (23%)
  Pallas kernels  19.5 us (21%)
  blocking collectives  14.4 us (16%)
  local copies, waits for them, and re-layouts  2.43 us (3%)
    ppermute x6, starting transfers between devices, send(): arrived.append(lax.ppermute(messages[shift], 'seq', onward[shift]))  16.7 us
    ppermute x6, starting transfers between devices, give_back(): home.append(lax.ppermute(results[shift], 'seq', back[shift]))  14 us
    ppermute x6, waiting for transfers between devices, send(): arrived.append(lax.ppermute(messages[shift], 'seq', onward[shift]))  11.8 us
    ppermute x6, waiting for transfers between devices, give_back(): home.append(lax.ppermute(results[shift], 'seq', back[shift]))  9.53 us
    all_gather x1, blocking collectives, exchanged_shards(): active_all = lax.all_gather(active, ('head', 'rep'), axis=0, tiled=True)  8.6 us
    all_gather x1, blocking collectives, exchanged_shards(): lift_all = lax.all_gather(lift_own, ('head', 'rep'), axis=0, tiled=True)  5.78 us
    pallas_call x1, Pallas kernels, first_layer(): pl.pallas_call(kernel, out_shape=[jax.ShapeDtypeStruct((own_channels, 6 *...  5.72 us
    pallas_call x2, Pallas kernels, attend(): pl.pallas_call(kernel, out_shape=[shape] * pieces, in_specs=whole_vmem(pi...  5.33 us
  transfers between devices with their start and end apart: 15, of which 4 were waited for; matrix products, arithmetic and copies ran while one was open for 2% of the time, Pallas kernels for 18%

commit v1 on v0

--- a/solution.py
+++ b/solution.py
@@ -189,6 +189,18 @@
     )
 
 
+def ring_of(chips):
+    return (0, 2, 3, 1) if chips == 4 else tuple(range(chips))
+
+
+def neighbour(chips, here, shift):
+    ring = ring_of(chips)
+    target = jnp.int32(0)
+    for at, chip in enumerate(ring):
+        target = jnp.where(here == chip, jnp.int32(ring[(at + shift) % chips]), target)
+    return target
+
+
 def whole_vmem(count):
     return [pl.BlockSpec(memory_space=pltpu.VMEM) for _ in range(count)]
 
@@ -211,12 +223,12 @@
     length = 3 * count * rows + tile_rows
 
     def kernel(*refs):
-        inputs, messages = (refs[: len(operands)], refs[len(operands) : -2])
-        blocks, sem = refs[-2:]
+        inputs, messages = (refs[: len(operands)], refs[len(operands) : len(operands) + chips])
+        blocks, sem, *extra = refs[len(operands) + chips :]
         here = lax.axis_index("seq")
         copies = []
         for shift in range(chips):
-            chip = lax.rem(here + shift, chips)
+            chip = neighbour(chips, here, shift)
             column = pl.multiple_of((chip * per_chip + first) * HEAD_DIM, HEAD_DIM)
             for kind in range(3):
                 copies.append(
@@ -227,11 +239,16 @@
                     )
                 )
         order = [3 * shift + kind for shift in list(range(1, chips)) + [0] for kind in range(3)]
+        if tile is not None:
+            tile_block, tile_sem = extra
+            tile_copy = pltpu.make_async_copy(inputs[3], tile_block, tile_sem)
+            tile_copy.start()
         for at in order:
             copies[at].start()
         if tile is not None:
             core = lax.axis_index("rep")
-            frames = [inputs[3][0, :, frame, :].astype(jnp.float32) for frame in range(2)]
+            tile_copy.wait()
+            frames = [tile_block[0, :, frame, :].astype(jnp.float32) for frame in range(2)]
             half = jnp.where(core == 0, frames[0], frames[1]).astype(jnp.bfloat16)
             for shift in range(chips):
                 messages[shift][pl.ds(3 * count * rows, tile_rows), :] = half
@@ -243,16 +260,18 @@
                     at, :, pl.ds(head * HEAD_DIM, HEAD_DIM)
                 ]
 
-    operands = [kept(source) for source in sources] + ([] if tile is None else [tile])
+    operands = [kept(source) for source in sources] + ([] if tile is None else [kept(tile)])
+    extra_scratch = [] if tile is None else [pltpu.VMEM(tile.shape, tile.dtype), pltpu.SemaphoreType.DMA]
     return pl.pallas_call(
         kernel,
         out_shape=[pltpu.VMEM((length, HEAD_DIM), jnp.bfloat16)] * chips,
-        in_specs=in_hbm(3) + ([] if tile is None else whole_vmem(1)),
+        in_specs=in_hbm(len(operands)),
         out_specs=whole_vmem(chips),
         scratch_shapes=[
             pltpu.VMEM((3 * chips, rows, count * HEAD_DIM), jnp.bfloat16),
             pltpu.SemaphoreType.DMA((3 * chips,)),
-        ],
+        ]
+        + extra_scratch,
         compiler_params=limit(12),
     )(*operands)
 
@@ -329,7 +348,7 @@
         squares = jnp.zeros((rows, HEAD_DIM), jnp.float32)
         for piece in range(pieces):
             base = pl.multiple_of(
-                lax.rem(here + piece, pieces) * (per_chip * HEAD_DIM), per_chip * HEAD_DIM
+                neighbour(pieces, here, piece) * (per_chip * HEAD_DIM), per_chip * HEAD_DIM
             )
             span = pl.ds(base, per_chip * HEAD_DIM)
             blocks = []
@@ -368,13 +387,14 @@
     return value / (1.0 + jnp.exp(-value))
 
 
-def store_shifted(windows, block, active):
+def store_shifted(windows, block, active, first, channels):
     depth, columns = active.shape
     lane = lax.broadcasted_iota(jnp.int32, (depth, columns), 1)
     before = jnp.where(lane == 0, 0.0, pltpu.roll(active, 1, 1))
     after = jnp.where(lane == columns - 1, 0.0, pltpu.roll(active, columns - 1, 1))
     for tap, window in enumerate((before, active, after)):
-        windows[pl.ds(tap * depth, depth), pl.ds(block * columns, columns)] = window.astype(jnp.bfloat16)
+        at = pl.ds(tap * channels + first, depth)
+        windows[at, pl.ds(block * columns, columns)] = window.astype(jnp.bfloat16)
 
 
 def frame_taps(weights, windows, frame_tap, width, in_rows, out_rows, totals):
@@ -415,7 +435,7 @@
             picked = jnp.zeros((latent, width), jnp.float32)
             for piece in range(chips):
                 tile = source[pl.ds(piece * latent, latent), :].astype(jnp.float32)
-                named = position_ref[lax.rem(row + chips - piece, chips)]
+                named = position_ref[neighbour(chips, row, -piece)]
                 picked = jnp.where(named == target, tile, picked)
             return picked
 
@@ -433,7 +453,7 @@
                     jnp.dot(weight_all, grid[frame][offset], preferred_element_type=jnp.float32) + bias_all
                 )
                 active = jnp.where(inside, silu(lifted), 0.0)
-                store_shifted(windows, frame * 5 + offset, active)
+                store_shifted(windows, frame * 5 + offset, active, 0, channels)
         weight_own = mine_ref[:, :latent].astype(jnp.bfloat16)
         bias_own = mine_ref[:, latent : latent + 1]
         totals = [jnp.zeros((own_channels, 3 * width), jnp.float32) for _ in range(2)]
@@ -472,13 +492,15 @@
     )(position, own_tiles, partner_tiles, lift_all, lift_own, kept(conv_weight))
 
 
-def second_layer(active, feature, conv_weight):
-    channels = active.shape[0]
-    width = active.shape[1] // 6
+def second_layer(blocks, feature, conv_weight):
     own_channels = feature.shape[0]
+    channels = own_channels * len(blocks)
+    width = blocks[0].shape[1] // 6
     taps = conv_weight.shape[1]
 
-    def kernel(active_ref, feature_ref, weight_ref, decoded_ref, weights, windows, sem):
+    def kernel(*refs):
+        inputs = refs[: len(blocks)]
+        feature_ref, weight_ref, decoded_ref, weights, windows, sem = refs[len(blocks) :]
         third = taps // 3
         copies = [
             pltpu.make_async_copy(
@@ -488,8 +510,13 @@
         ]
         for copy in copies:
             copy.start()
-        for block in range(6):
-            store_shifted(windows, block, active_ref[:, pl.ds(block * width, width)].astype(jnp.float32))
+        at = 2 * lax.axis_index("head") + lax.axis_index("rep")
+        for index, source in enumerate(inputs):
+            first = pl.multiple_of(jnp.bitwise_xor(at, index) * own_channels, own_channels)
+            for block in range(6):
+                store_shifted(
+                    windows, block, source[:, pl.ds(block * width, width)].astype(jnp.float32), first, channels
+                )
         totals = [jnp.zeros((own_channels, width), jnp.float32) for _ in range(2)]
         for frame_tap in range(3):
             copies[frame_tap].wait()
@@ -500,7 +527,7 @@
     return pl.pallas_call(
         kernel,
         out_shape=jax.ShapeDtypeStruct((own_channels, 2, width), jnp.float32),
-        in_specs=whole_vmem(2) + in_hbm(1),
+        in_specs=whole_vmem(len(blocks) + 1) + in_hbm(1),
         out_specs=pl.BlockSpec(memory_space=pltpu.VMEM),
         scratch_shapes=[
             pltpu.VMEM((taps, own_channels, channels), jnp.bfloat16),
@@ -509,7 +536,7 @@
         ],
         compiler_params=limit(16),
         name="second_layer",
-    )(active, feature, kept(conv_weight))
+    )(*blocks, feature, kept(conv_weight))
 
 
 def exchanged_shards(
@@ -530,26 +557,21 @@
     per_chip = queries.shape[1] // HEAD_DIM // chips
     count = per_chip // 2
     latent_channels = tile_pool.shape[1]
-    onward = [[(i, (i + shift) % chips) for i in range(chips)] for shift in range(chips)]
-    back = [[(j, i) for i, j in pairs] for pairs in onward]
+    ring = ring_of(chips)
+    onward = [[(ring[at], ring[(at + shift) % chips]) for at in range(chips)] for shift in range(chips)]
+    back = [[(target, source) for source, target in pairs] for pairs in onward]
     swap = [(0, 1), (1, 0)]
     sources = (queries, key_tokens, value_tokens)
 
-    def send(messages):
+    def send(messages, permutations):
         arrived = [messages[0]]
         for shift in range(1, chips):
-            arrived.append(lax.ppermute(messages[shift], "seq", onward[shift]))
+            arrived.append(lax.ppermute(messages[shift], "seq", permutations[shift]))
         return arrived
-
-    def give_back(results):
-        home = [results[0]]
-        for shift in range(1, chips):
-            home.append(lax.ppermute(results[shift], "seq", back[shift]))
-        return home
 
     early = pack(sources, tile_pool, chips, per_chip, 0, count)
     late = pack(sources, None, chips, per_chip, count, count)
-    early_in, late_in = (send(early), send(late))
+    early_in, late_in = (send(early, onward), send(late, onward))
 
     lift_weight, lift_bias, _ = lax.optimization_barrier((lift_weight, lift_bias, late[0]))
     lift_own = jnp.concatenate(
@@ -566,21 +588,21 @@
     own = join(early_in, count, rows, latent_channels)
     partner = lax.ppermute(own, "rep", swap)
     tiles_at = 2 * count * chips * rows
+    active, feature = first_layer(tile_position, own[tiles_at:], partner[tiles_at:], lift_all, lift_own, conv_weight)
+    core_active = lax.ppermute(active, "rep", swap)
+    chip_active = lax.ppermute(active, "head", swap)
     early_out = attend(early_in, own, partner, count, rows)
-    early_home = give_back(early_out)
-
-    own, partner, _ = lax.optimization_barrier((own, partner, early_out[0]))
-    active, feature = first_layer(tile_position, own[tiles_at:], partner[tiles_at:], lift_all, lift_own, conv_weight)
-    active_all = lax.all_gather(active, ("head", "rep"), axis=0, tiled=True)
-
-    late_in, active_all = lax.optimization_barrier((late_in, active_all))
+    early_home = send(early_out, back)
+
+    late_in, _ = lax.optimization_barrier((late_in, early_out[0]))
     own = join(late_in, count, rows, 0)
     partner = lax.ppermute(own, "rep", swap)
     late_out = attend(late_in, own, partner, count, rows)
-    late_home = give_back(late_out)
-
-    active_all, _ = lax.optimization_barrier((active_all, late_out[0]))
-    decoded = second_layer(active_all, feature, conv_weight)
+    late_home = send(late_out, back)
+
+    chip_active, _ = lax.optimization_barrier((chip_active, late_out[0]))
+    far_active = lax.ppermute(chip_active, "rep", swap)
+    decoded = second_layer((active, core_active, chip_active, far_active), feature, conv_weight)
     decoded = decoded[:, :, None, :]
 
     hidden, part = close(

time: 91.9 us -> 98.5 us (1.072)
  waiting for transfers between devices: 21.3 us -> 48.7 us
  starting transfers between devices: 32.3 us -> 20.8 us
  blocking collectives: 14.4 us -> 5.78 us
    ppermute x12 -> x15, waiting for transfers between devices: 21.3 us -> 45.8 us  [the longest x12 45.8 us: send(): arrived.append(lax.ppermute(messages[shift], 'seq', permutations[shift]))]
    ppermute x12 -> x15, starting transfers between devices: 30.7 us -> 20.1 us  [the longest x12 18 us: send(): arrived.append(lax.ppermute(messages[shift], 'seq', permutations[shift]))]
    all_gather x1 -> x0, blocking collectives: 8.6 us -> none  [exchanged_shards(): active_all = lax.all_gather(active, ('head', 'rep'), axis=0, tiled=True)]
    ppermute x1, waiting for transfers between devices: 0.01 us -> 2.91 us  [exchanged_shards(): part = part + lax.ppermute(part, 'head', swap)]
  transfers between devices with their start and end apart: 15 -> 18, of which waited for: 4 -> 7; matrix products, arithmetic and copies ran while one was open for 2% -> 2% of each run, Pallas kernels for 18% -> 14%
where the time goes in v1:
time: 98.5 us; the launch traced here: 98.2 us
  waiting for transfers between devices  48.7 us (49%)
  starting transfers between devices  20.8 us (21%)
  Pallas kernels  19.6 us (20%)
  blocking collectives  5.78 us (6%)
  local copies, waits for them, and re-layouts  1.67 us (2%)
    ppermute x12, waiting for transfers between devices, send(): arrived.append(lax.ppermute(messages[shift], 'seq', permutations[shift]))  45.8 us
    ppermute x12, starting transfers between devices, send(): arrived.append(lax.ppermute(messages[shift], 'seq', permutations[shift]))  18 us
    all_gather x1, blocking collectives, exchanged_shards(): lift_all = lax.all_gather(lift_own, ('head', 'rep'), axis=0, tiled=True)  5.78 us
    pallas_call x1, Pallas kernels, first_layer(): pl.pallas_call(kernel, out_shape=[jax.ShapeDtypeStruct((own_channels, 6 *...  5.64 us
    pallas_call x2, Pallas kernels, attend(): pl.pallas_call(kernel, out_shape=[shape] * pieces, in_specs=whole_vmem(pi...  5.3 us
    pallas_call x1, Pallas kernels, second_layer(): pl.pallas_call(kernel, out_shape=jax.ShapeDtypeStruct((own_channels, 2, w...  4.14 us
    pallas_call x2, Pallas kernels, pack(): pl.pallas_call(kernel, out_shape=[pltpu.VMEM((length, HEAD_DIM), jnp.bflo...  3.08 us
    ppermute x1, waiting for transfers between devices, exchanged_shards(): part = part + lax.ppermute(part, 'head', swap)  2.91 us
  transfers between devices with their start and end apart: 18, of which 7 were waited for; matrix products, arithmetic and copies ran while one was open for 2% of the time, Pallas kernels for 14%

profile of v1, /device:TPU:0, one launch (start us, length us, event | category | flops | bytes accessed | tf_op | source)
XLA Modules:
  0.0 98.2 jit_solution(13732826130471041252)
XLA Ops:
  0.6 1.6 %shard_map.130 = (bf16[1216,128]{1,0:T(8,128)(2,1)S(1)}, bf16[1216,128]{1,0:T(8,128)(2,1)S(1)}, bf16[1216,128]{1,0:T(8,128)(2,1)S(1)}, bf16[1216,128]{1,0:T(8,128)(2,1)S(1)}) custom-call(bf16[128,3072]{1,0:T(8,128)(2,1)} %refs_0_.3, bf16[128,3072]{1,0:T(8,128)(2,1)} %refs_1_.3, bf16[128,3072]{1,0:T(8,128)(2,1)} %refs_2_.3, bf16[1,64,2,128]{3,2,1,0:T(2,128)(2,1)} %refs_3_.1), custom_call_target="tpu_custom_call" | custom-call | tf_op jit(solution)/shard_map/pallas_call | solution.py:265
  2.3 4.1 %collective-permute-start = (bf16[1216,128]{1,0:T(8,128)(2,1)S(1)}, bf16[1216,128]{1,0:T(8,128)(2,1)S(1)}, u32[]{:S(2)}, u32[]{:S(2)}) collective-permute-start(bf16[1216,128]{1,0:T(8,128)(2,1)S(1)} %get-tuple-element.36), channel_id=1, source_target_pairs={{0,8},{8,12},{12,4},{4,0},{1,9},{9,13},{13,5},{5,1},{2,10},{10,14}... | collective-permute-start | bytes 933896 | tf_op jit(solution)/shard_map/ppermute | solution.py:569
  6.4 1.3 %collective-permute-start.1 = (bf16[1216,128]{1,0:T(8,128)(2,1)S(1)}, bf16[1216,128]{1,0:T(8,128)(2,1)S(1)}, u32[]{:S(2)}, u32[]{:S(2)}) collective-permute-start(bf16[1216,128]{1,0:T(8,128)(2,1)S(1)} %get-tuple-element.37), channel_id=1, source_target_pairs={{0,12},{8,4},{12,0},{4,8},{1,13},{9,5},{13,1},{5,9},{2,14},{10,6},... | collective-permute-start | bytes 933896 | tf_op jit(solution)/shard_map/ppermute | solution.py:569
  7.7 0.8 collective-permute-start.2
  8.5 1.5 %shard_map.131 = (bf16[1152,128]{1,0:T(8,128)(2,1)S(1)}, bf16[1152,128]{1,0:T(8,128)(2,1)S(1)}, bf16[1152,128]{1,0:T(8,128)(2,1)S(1)}, bf16[1152,128]{1,0:T(8,128)(2,1)S(1)}) custom-call(bf16[128,3072]{1,0:T(8,128)(2,1)} %refs_0_.3, bf16[128,3072]{1,0:T(8,128)(2,1)} %refs_1_.3, bf16[128,3072]{1,0:T(8,128)(2,1)} %refs_2_.3), custom_call_target="tpu_custom_call" | custom-call | tf_op jit(solution)/shard_map/pallas_call | solution.py:265
  10.0 0.8 copy.18
  10.8 0.8 copy.17
  11.7 5.8 %all_gather.3.all_ref = f32[512,128]{1,0:T(8,128)S(1)} all-gather(f32[128,128]{1,0:T(8,128)S(1)} %maximum_maximum_fusion.mine_ref), channel_id=1, replica_groups=mesh['groups'=2,'seq'=4,'head'=2,'rep'=2] {'head','rep'}, dimensions={0}, use_global_device_ids=true | all-gather | bytes 327680 | tf_op jit(solution)/shard_map/all_gather | solution.py:585
  17.5 5.1 %collective-permute-done.1.refs_2_ = bf16[1216,128]{1,0:T(8,128)(2,1)S(1)} collective-permute-done((bf16[1216,128]{1,0:T(8,128)(2,1)S(1)}, bf16[1216,128]{1,0:T(8,128)(2,1)S(1)}, u32[]{:S(2)}, u32[]{:S(2)}) %collective-permute-start.1) | collective-permute-done | bytes 311328 | tf_op jit(solution)/shard_map/ppermute | solution.py:569
  22.7 12.2 %collective-permute-done.2.refs_3_ = bf16[1216,128]{1,0:T(8,128)(2,1)S(1)} collective-permute-done((bf16[1216,128]{1,0:T(8,128)(2,1)S(1)}, bf16[1216,128]{1,0:T(8,128)(2,1)S(1)}, u32[]{:S(2)}, u32[]{:S(2)}) %collective-permute-start.2) | collective-permute-done | bytes 311328 | tf_op jit(solution)/shard_map/ppermute | solution.py:569
  35.0 2.5 %collective-permute-start.8 = (bf16[1152,128]{1,0:T(8,128)(2,1)S(1)}, bf16[1152,128]{1,0:T(8,128)(2,1)S(1)}, u32[]{:S(2)}, u32[]{:S(2)}) collective-permute-start(bf16[1152,128]{1,0:T(8,128)(2,1)S(1)} %get-tuple-element.51), channel_id=1, source_target_pairs={{0,12},{8,4},{12,0},{4,8},{1,13},{9,5},{13,1},{5,9},{2,14},{10,6},... | collective-permute-start | bytes 884744 | tf_op jit(solution)/shard_map/ppermute | solution.py:569
  37.6 1.0 %collective-permute-start.9 = (bf16[1152,128]{1,0:T(8,128)(2,1)S(1)}, bf16[1152,128]{1,0:T(8,128)(2,1)S(1)}, u32[]{:S(2)}, u32[]{:S(2)}) collective-permute-start(bf16[1152,128]{1,0:T(8,128)(2,1)S(1)} %get-tuple-element.52), channel_id=1, source_target_pairs={{0,4},{8,0},{12,8},{4,12},{1,5},{9,1},{13,9},{5,13},{2,6},{10,2},{... | collective-permute-start | bytes 884744 | tf_op jit(solution)/shard_map/ppermute | solution.py:569
  38.6 2.6 %shard_map.133 = (bf16[384,128]{1,0:T(8,128)(2,1)S(1)}, bf16[384,128]{1,0:T(8,128)(2,1)S(1)}, bf16[384,128]{1,0:T(8,128)(2,1)S(1)}, bf16[384,128]{1,0:T(8,128)(2,1)S(1)}) custom-call(bf16[1216,128]{1,0:T(8,128)(2,1)S(1)} %get-tuple-element.42.refs_0_, bf16[1216,128]{1,0:T(8,128)(2,1)S(1)} %collective-permute-done.refs_1_, ...), custom_call_target="tpu_custom_call" | custom-call | tf_op jit(solution)/shard_map/pallas_call | solution.py:328
  41.3 3.1 %collective-permute-done.7.refs_1_ = bf16[1152,128]{1,0:T(8,128)(2,1)S(1)} collective-permute-done((bf16[1152,128]{1,0:T(8,128)(2,1)S(1)}, bf16[1152,128]{1,0:T(8,128)(2,1)S(1)}, u32[]{:S(2)}, u32[]{:S(2)}) %collective-permute-start.7) | collective-permute-done | bytes 294944 | tf_op jit(solution)/shard_map/ppermute | solution.py:569
  44.4 7.3 %collective-permute-done.8.refs_2_ = bf16[1152,128]{1,0:T(8,128)(2,1)S(1)} collective-permute-done((bf16[1152,128]{1,0:T(8,128)(2,1)S(1)}, bf16[1152,128]{1,0:T(8,128)(2,1)S(1)}, u32[]{:S(2)}, u32[]{:S(2)}) %collective-permute-start.8) | collective-permute-done | bytes 294944 | tf_op jit(solution)/shard_map/ppermute | solution.py:569
  51.7 12.3 %collective-permute-done.9.refs_3_ = bf16[1152,128]{1,0:T(8,128)(2,1)S(1)} collective-permute-done((bf16[1152,128]{1,0:T(8,128)(2,1)S(1)}, bf16[1152,128]{1,0:T(8,128)(2,1)S(1)}, u32[]{:S(2)}, u32[]{:S(2)}) %collective-permute-start.9) | collective-permute-done | bytes 294944 | tf_op jit(solution)/shard_map/ppermute | solution.py:569
  64.1 0.1 collective-permute-start.10
  64.3 1.4 %collective-permute-start.5 = (bf16[384,128]{1,0:T(8,128)(2,1)S(1)}, bf16[384,128]{1,0:T(8,128)(2,1)S(1)}, u32[]{:S(2)}, u32[]{:S(2)}) collective-permute-start(bf16[384,128]{1,0:T(8,128)(2,1)S(1)} %get-tuple-element.48), channel_id=1, source_target_pairs={{12,0},{4,8},{0,12},{8,4},{13,1},{5,9},{1,13},{9,5},{14,2},{6,10},... | collective-permute-start | bytes 294920 | tf_op jit(solution)/shard_map/ppermute | solution.py:569
  65.7 5.6 %first_layer.1 = (bf16[128,768]{1,0:T(8,128)(2,1)S(1)}, f32[128,256]{1,0:T(8,128)S(1)}) custom-call(s32[4]{0:T(128)S(1)} %copy-done.3, bf16[256,128]{1,0:T(8,128)(2,1)S(1)} %slice.18.own_ref, bf16[256,128]{1,0:T(8,128)(2,1)S(1)} %slice.19.partner_ref, f32[512,128]{1,0:T(8,128)S(1)} %all_gather.3.all_ref, f32[128,128]{1,0:T(8,128)S(1)} %maximum_maximum_fusion.mine_ref, ...), custom_call_target="tpu_custom_call" | custom-call | tf_op jit(solution)/shard_map/first_layer/pallas_call | solution.py:477
  71.3 1.6 %collective-permute-start.16 = (bf16[128,768]{1,0:T(8,128)(2,1)S(1)}, bf16[128,768]{1,0:T(8,128)(2,1)S(1)}, u32[]{:S(2)}, u32[]{:S(2)}) collective-permute-start(bf16[128,768]{1,0:T(8,128)(2,1)S(1)} %get-tuple-element.64.refs_0_), channel_id=1, source_target_pairs={{0,2},{2,0},{1,3},{3,1},{4,6},{6,4},{5,7},{7,5},{8,10},{10,8},{9,1... | collective-permute-start | bytes 589832 | tf_op jit(solution)/shard_map/ppermute | solution.py:593
  72.9 2.0 %collective-permute-start.6 = (bf16[384,128]{1,0:T(8,128)(2,1)S(1)}, bf16[384,128]{1,0:T(8,128)(2,1)S(1)}, u32[]{:S(2)}, u32[]{:S(2)}) collective-permute-start(bf16[384,128]{1,0:T(8,128)(2,1)S(1)} %get-tuple-element.49), channel_id=1, source_target_pairs={{4,0},{0,8},{8,12},{12,4},{5,1},{1,9},{9,13},{13,5},{6,2},{2,10},{... | collective-permute-start | bytes 294920 | tf_op jit(solution)/shard_map/ppermute | solution.py:569
  74.9 2.6 %shard_map.135 = (bf16[384,128]{1,0:T(8,128)(2,1)S(1)}, bf16[384,128]{1,0:T(8,128)(2,1)S(1)}, bf16[384,128]{1,0:T(8,128)(2,1)S(1)}, bf16[384,128]{1,0:T(8,128)(2,1)S(1)}) custom-call(bf16[1152,128]{1,0:T(8,128)(2,1)S(1)} %get-tuple-element.53.refs_0_, bf16[1152,128]{1,0:T(8,128)(2,1)S(1)} %collective-permute-done.7.refs_1_, ...), custom_call_target="tpu_custom_call" | custom-call | tf_op jit(solution)/shard_map/pallas_call | solution.py:328
  77.5 0.4 collective-permute-start.11
  77.9 2.4 %collective-permute-start.12 = (bf16[384,128]{1,0:T(8,128)(2,1)S(1)}, bf16[384,128]{1,0:T(8,128)(2,1)S(1)}, u32[]{:S(2)}, u32[]{:S(2)}) collective-permute-start(bf16[384,128]{1,0:T(8,128)(2,1)S(1)} %get-tuple-element.59), channel_id=1, source_target_pairs={{12,0},{4,8},{0,12},{8,4},{13,1},{5,9},{1,13},{9,5},{14,2},{6,10},... | collective-permute-start | bytes 294920 | tf_op jit(solution)/shard_map/ppermute | solution.py:569
  80.3 1.9 %collective-permute-start.13 = (bf16[384,128]{1,0:T(8,128)(2,1)S(1)}, bf16[384,128]{1,0:T(8,128)(2,1)S(1)}, u32[]{:S(2)}, u32[]{:S(2)}) collective-permute-start(bf16[384,128]{1,0:T(8,128)(2,1)S(1)} %get-tuple-element.60), channel_id=1, source_target_pairs={{4,0},{0,8},{8,12},{12,4},{5,1},{1,9},{9,13},{13,5},{6,2},{2,10},{... | collective-permute-start | bytes 294920 | tf_op jit(solution)/shard_map/ppermute | solution.py:569
  82.2 5.7 %collective-permute-done.11.refs_5_ = bf16[384,128]{1,0:T(8,128)(2,1)S(1)} collective-permute-done((bf16[384,128]{1,0:T(8,128)(2,1)S(1)}, bf16[384,128]{1,0:T(8,128)(2,1)S(1)}, u32[]{:S(2)}, u32[]{:S(2)}) %collective-permute-start.11) | collective-permute-done | bytes 98336 | tf_op jit(solution)/shard_map/ppermute | solution.py:569
  88.0 1.3 %close.1 = (bf16[128,3072]{1,0:T(8,128)(2,1)}, f32[72,128]{1,0:T(8,128)S(1)}) custom-call(bf16[384,128]{1,0:T(8,128)(2,1)S(1)} %get-tuple-element.46.refs_0_, bf16[384,128]{1,0:T(8,128)(2,1)S(1)} %collective-permute-done.4.refs_1_, bf16[384,128]{1,0:T(8,128)(2,1)S(1)} %collective-permute-done.5.refs_2_, bf16[384,128]{1,0:T(8,128)(2,1)S(1)} %collective-permute-done.6.refs_3_, ...), custom_call_target="tpu_custom_call" | custom-call | tf_op jit(solution)/shard_map/close/pallas_call | solution.py:373
  89.3 0.5 collective-permute-start.14
  89.9 0.5 collective-permute-start.17
  90.4 2.9 %collective-permute-done.14 = f32[72,128]{1,0:T(8,128)S(1)} collective-permute-done((f32[72,128]{1,0:T(8,128)S(1)}, f32[72,128]{1,0:T(8,128)S(1)}, u32[]{:S(2)}, u32[]{:S(2)}) %collective-permute-start.14) | collective-permute-done | bytes 36896 | tf_op jit(solution)/shard_map/ppermute | solution.py:611
  93.3 0.6 fusion
  93.9 4.1 %second_layer.1 = f32[128,2,128]{2,1,0:T(2,128)} custom-call(bf16[128,768]{1,0:T(8,128)(2,1)S(1)} %get-tuple-element.64.refs_0_, bf16[128,768]{1,0:T(8,128)(2,1)S(1)} %collective-permute-done.15.refs_1_, bf16[128,768]{1,0:T(8,128)(2,1)S(1)} %collective-permute-done.16.refs_2_, bf16[128,768]{1,0:T(8,128)(2,1)S(1)} %collective-permute-done.17.refs_3_, ...), custom_call_target="tpu_custom_call" | custom-call | tf_op jit(solution)/shard_map/second_layer/pallas_call | solution.py:527
  (32 shorter events, 0.5 us)
Async XLA Ops:
  0.6 65.1 %copy-start.3 = (s32[4]{0:T(128)S(1)}, s32[4]{0:T(128)}, u32[]{:S(2)}) copy-start(s32[4]{0:T(128)} %position_ref.1) | copy-start | bytes 52
  2.3 15.3 %collective-permute-start = (bf16[1216,128]{1,0:T(8,128)(2,1)S(1)}, bf16[1216,128]{1,0:T(8,128)(2,1)S(1)}, u32[]{:S(2)}, u32[]{:S(2)}) collective-permute-start(bf16[1216,128]{1,0:T(8,128)(2,1)S(1)} %get-tuple-element.36), channel_id=1, source_target_pairs={{0,8},{8,12},{12,4},{4,0},{1,9},{9,13},{13,5},{5,1},{2,10},{10,14}... | collective-permute-start | bytes 933896 | tf_op jit(solution)/shard_map/ppermute | solution.py:569
  6.4 16.3 %collective-permute-start.1 = (bf16[1216,128]{1,0:T(8,128)(2,1)S(1)}, bf16[1216,128]{1,0:T(8,128)(2,1)S(1)}, u32[]{:S(2)}, u32[]{:S(2)}) collective-permute-start(bf16[1216,128]{1,0:T(8,128)(2,1)S(1)} %get-tuple-element.37), channel_id=1, source_target_pairs={{0,12},{8,4},{12,0},{4,8},{1,13},{9,5},{13,1},{5,9},{2,14},{10,6},... | collective-permute-start | bytes 933896 | tf_op jit(solution)/shard_map/ppermute | solution.py:569
  7.7 27.1 %collective-permute-start.2 = (bf16[1216,128]{1,0:T(8,128)(2,1)S(1)}, bf16[1216,128]{1,0:T(8,128)(2,1)S(1)}, u32[]{:S(2)}, u32[]{:S(2)}) collective-permute-start(bf16[1216,128]{1,0:T(8,128)(2,1)S(1)} %get-tuple-element.38), channel_id=1, source_target_pairs={{0,4},{8,0},{12,8},{4,12},{1,5},{9,1},{13,9},{5,13},{2,6},{10,2},{... | collective-permute-start | bytes 933896 | tf_op jit(solution)/shard_map/ppermute | solution.py:569
  34.9 3.7 %collective-permute-start.3 = (bf16[3328,128]{1,0:T(8,128)(2,1)S(1)}, bf16[3328,128]{1,0:T(8,128)(2,1)S(1)}, u32[]{:S(2)}, u32[]{:S(2)}) collective-permute-start(bf16[3328,128]{1,0:T(8,128)(2,1)S(1)} %shard_map.132.refs_4_), channel_id=1, source_target_pairs={{0,1},{1,0},{2,3},{3,2},{4,5},{5,4},{6,7},{7,6},{8,9},{9,8},{10,11... | collective-permute-start | bytes 2555912 | tf_op jit(solution)/shard_map/ppermute | solution.py:589
  35.0 9.4 %collective-permute-start.7 = (bf16[1152,128]{1,0:T(8,128)(2,1)S(1)}, bf16[1152,128]{1,0:T(8,128)(2,1)S(1)}, u32[]{:S(2)}, u32[]{:S(2)}) collective-permute-start(bf16[1152,128]{1,0:T(8,128)(2,1)S(1)} %get-tuple-element.50), channel_id=1, source_target_pairs={{0,8},{8,12},{12,4},{4,0},{1,9},{9,13},{13,5},{5,1},{2,10},{10,14}... | collective-permute-start | bytes 884744 | tf_op jit(solution)/shard_map/ppermute | solution.py:569
  35.0 16.7 %collective-permute-start.8 = (bf16[1152,128]{1,0:T(8,128)(2,1)S(1)}, bf16[1152,128]{1,0:T(8,128)(2,1)S(1)}, u32[]{:S(2)}, u32[]{:S(2)}) collective-permute-start(bf16[1152,128]{1,0:T(8,128)(2,1)S(1)} %get-tuple-element.51), channel_id=1, source_target_pairs={{0,12},{8,4},{12,0},{4,8},{1,13},{9,5},{13,1},{5,9},{2,14},{10,6},... | collective-permute-start | bytes 884744 | tf_op jit(solution)/shard_map/ppermute | solution.py:569
  37.6 50.4 %copy-start = (bf16[128,3072]{1,0:T(8,128)(2,1)S(1)}, bf16[128,3072]{1,0:T(8,128)(2,1)}, u32[]{:S(2)}) copy-start(bf16[128,3072]{1,0:T(8,128)(2,1)} %refs_8_.1) | copy-start | bytes 2359300
  37.6 50.4 %copy-start.1 = (bf16[3072,64]{0,1:T(8,128)(2,1)S(1)}, bf16[3072,64]{0,1:T(8,128)(2,1)}, u32[]{:S(2)}) copy-start(bf16[3072,64]{0,1:T(8,128)(2,1)} %param.16) | copy-start | bytes 1179652
  37.6 50.4 %copy-start.2 = (f32[3072]{0:T(1024)S(1)}, f32[3072]{0:T(1024)}, u32[]{:S(2)}) copy-start(f32[3072]{0:T(1024)} %param.15) | copy-start | bytes 36868
  37.6 26.5 %collective-permute-start.9 = (bf16[1152,128]{1,0:T(8,128)(2,1)S(1)}, bf16[1152,128]{1,0:T(8,128)(2,1)S(1)}, u32[]{:S(2)}, u32[]{:S(2)}) collective-permute-start(bf16[1152,128]{1,0:T(8,128)(2,1)S(1)} %get-tuple-element.52), channel_id=1, source_target_pairs={{0,4},{8,0},{12,8},{4,12},{1,5},{9,1},{13,9},{5,13},{2,6},{10,2},{... | collective-permute-start | bytes 884744 | tf_op jit(solution)/shard_map/ppermute | solution.py:569
  64.1 10.7 %collective-permute-start.10 = (bf16[3072,128]{1,0:T(8,128)(2,1)S(1)}, bf16[3072,128]{1,0:T(8,128)(2,1)S(1)}, u32[]{:S(2)}, u32[]{:S(2)}) collective-permute-start(bf16[3072,128]{1,0:T(8,128)(2,1)S(1)} %shard_map.134.refs_4_), channel_id=1, source_target_pairs={{0,1},{1,0},{2,3},{3,2},{4,5},{5,4},{6,7},{7,6},{8,9},{9,8},{10,11... | collective-permute-start | bytes 2359304 | tf_op jit(solution)/shard_map/ppermute | solution.py:599
  64.2 13.6 %collective-permute-start.4 = (bf16[384,128]{1,0:T(8,128)(2,1)S(1)}, bf16[384,128]{1,0:T(8,128)(2,1)S(1)}, u32[]{:S(2)}, u32[]{:S(2)}) collective-permute-start(bf16[384,128]{1,0:T(8,128)(2,1)S(1)} %get-tuple-element.47), channel_id=1, source_target_pairs={{8,0},{12,8},{4,12},{0,4},{9,1},{13,9},{5,13},{1,5},{10,2},{14,10}... | collective-permute-start | bytes 294920 | tf_op jit(solution)/shard_map/ppermute | solution.py:569
  64.3 16.0 %collective-permute-start.5 = (bf16[384,128]{1,0:T(8,128)(2,1)S(1)}, bf16[384,128]{1,0:T(8,128)(2,1)S(1)}, u32[]{:S(2)}, u32[]{:S(2)}) collective-permute-start(bf16[384,128]{1,0:T(8,128)(2,1)S(1)} %get-tuple-element.48), channel_id=1, source_target_pairs={{12,0},{4,8},{0,12},{8,4},{13,1},{5,9},{1,13},{9,5},{14,2},{6,10},... | collective-permute-start | bytes 294920 | tf_op jit(solution)/shard_map/ppermute | solution.py:569
  71.3 18.5 %collective-permute-start.16 = (bf16[128,768]{1,0:T(8,128)(2,1)S(1)}, bf16[128,768]{1,0:T(8,128)(2,1)S(1)}, u32[]{:S(2)}, u32[]{:S(2)}) collective-permute-start(bf16[128,768]{1,0:T(8,128)(2,1)S(1)} %get-tuple-element.64.refs_0_), channel_id=1, source_target_pairs={{0,2},{2,0},{1,3},{3,1},{4,6},{6,4},{5,7},{7,5},{8,10},{10,8},{9,1... | collective-permute-start | bytes 589832 | tf_op jit(solution)/shard_map/ppermute | solution.py:593
  72.9 9.4 %collective-permute-start.6 = (bf16[384,128]{1,0:T(8,128)(2,1)S(1)}, bf16[384,128]{1,0:T(8,128)(2,1)S(1)}, u32[]{:S(2)}, u32[]{:S(2)}) collective-permute-start(bf16[384,128]{1,0:T(8,128)(2,1)S(1)} %get-tuple-element.49), channel_id=1, source_target_pairs={{4,0},{0,8},{8,12},{12,4},{5,1},{1,9},{9,13},{13,5},{6,2},{2,10},{... | collective-permute-start | bytes 294920 | tf_op jit(solution)/shard_map/ppermute | solution.py:569
  77.5 10.4 %collective-permute-start.11 = (bf16[384,128]{1,0:T(8,128)(2,1)S(1)}, bf16[384,128]{1,0:T(8,128)(2,1)S(1)}, u32[]{:S(2)}, u32[]{:S(2)}) collective-permute-start(bf16[384,128]{1,0:T(8,128)(2,1)S(1)} %get-tuple-element.58), channel_id=1, source_target_pairs={{8,0},{12,8},{4,12},{0,4},{9,1},{13,9},{5,13},{1,5},{10,2},{14,10}... | collective-permute-start | bytes 294920 | tf_op jit(solution)/shard_map/ppermute | solution.py:569
  77.9 10.1 %collective-permute-start.12 = (bf16[384,128]{1,0:T(8,128)(2,1)S(1)}, bf16[384,128]{1,0:T(8,128)(2,1)S(1)}, u32[]{:S(2)}, u32[]{:S(2)}) collective-permute-start(bf16[384,128]{1,0:T(8,128)(2,1)S(1)} %get-tuple-element.59), channel_id=1, source_target_pairs={{12,0},{4,8},{0,12},{8,4},{13,1},{5,9},{1,13},{9,5},{14,2},{6,10},... | collective-permute-start | bytes 294920 | tf_op jit(solution)/shard_map/ppermute | solution.py:569
  80.3 7.6 %collective-permute-start.13 = (bf16[384,128]{1,0:T(8,128)(2,1)S(1)}, bf16[384,128]{1,0:T(8,128)(2,1)S(1)}, u32[]{:S(2)}, u32[]{:S(2)}) collective-permute-start(bf16[384,128]{1,0:T(8,128)(2,1)S(1)} %get-tuple-element.60), channel_id=1, source_target_pairs={{4,0},{0,8},{8,12},{12,4},{5,1},{1,9},{9,13},{13,5},{6,2},{2,10},{... | collective-permute-start | bytes 294920 | tf_op jit(solution)/shard_map/ppermute | solution.py:569
  89.3 4.0 %collective-permute-start.14 = (f32[72,128]{1,0:T(8,128)S(1)}, f32[72,128]{1,0:T(8,128)S(1)}, u32[]{:S(2)}, u32[]{:S(2)}) collective-permute-start(f32[72,128]{1,0:T(8,128)S(1)} %get-tuple-element.62), channel_id=1, source_target_pairs={{0,2},{2,0},{1,3},{3,1},{4,6},{6,4},{5,7},{7,5},{8,10},{10,8},{9,1... | collective-permute-start | bytes 110600 | tf_op jit(solution)/shard_map/ppermute | solution.py:611
  89.8 4.1 %collective-permute-start.15 = (bf16[128,768]{1,0:T(8,128)(2,1)S(1)}, bf16[128,768]{1,0:T(8,128)(2,1)S(1)}, u32[]{:S(2)}, u32[]{:S(2)}) collective-permute-start(bf16[128,768]{1,0:T(8,128)(2,1)S(1)} %get-tuple-element.64.refs_0_), channel_id=1, source_target_pairs={{0,1},{1,0},{2,3},{3,2},{4,5},{5,4},{6,7},{7,6},{8,9},{9,8},{10,11... | collective-permute-start | bytes 589832 | tf_op jit(solution)/shard_map/ppermute | solution.py:592
  89.9 4.1 %collective-permute-start.17 = (bf16[128,768]{1,0:T(8,128)(2,1)S(1)}, bf16[128,768]{1,0:T(8,128)(2,1)S(1)}, u32[]{:S(2)}, u32[]{:S(2)}) collective-permute-start(bf16[128,768]{1,0:T(8,128)(2,1)S(1)} %collective-permute-done.16.refs_2_), channel_id=1, source_target_pairs={{0,1},{1,0},{2,3},{3,2},{4,5},{5,4},{6,7},{7,6},{8,9},{9,8},{10,11... | collective-permute-start | bytes 589832 | tf_op jit(solution)/shard_map/ppermute | solution.py:604
